TPU v7x, 32 devices: a whole 2x2x4 slice. The times are simulated.
32 devices in a mesh: dp: 4 (over x, core), fsdp: 2 (over y), tensor: 4 (over z).
Axes of the slice: x: 2, y: 2, z: 4, core: 2. Of those that a mesh axis runs over, the one named last changes fastest.
Arguments:
- tokens: bfloat16 [8, 768, 8192], P(('dp', 'fsdp'), 'tensor'), may hold values from -6 to 6
- norm_gain: float32 [8192], replicated, may hold values from 0.85 to 4
- w_qkv: bfloat16 [8192, 5120], P(('dp', 'fsdp'), 'tensor'), may hold values from -0.3 to 0.3
- a_query: bfloat16 [8192, 16], replicated, may hold values from -0.0625 to 0.0625
- query_up_adapter: bfloat16 [16, 4096], P(None, 'tensor'), may hold values from -1.5 to 1.5
- a_value: bfloat16 [8192, 16], replicated, may hold values from -0.0625 to 0.0625
- value_up_adapter: bfloat16 [16, 512], P(None, 'tensor'), may hold values from -1.5 to 1.5
- out_grad: bfloat16 [8, 768, 4096], P(('dp', 'fsdp'), 'tensor'), may hold values from -6 to 6
Outputs:
- attn_out: bfloat16 [8, 768, 4096], P(('dp', 'fsdp'), 'tensor')
- grad_a_query: float32 [8192, 16], replicated
- grad_b_query: float32 [16, 4096], P(None, 'tensor')
- grad_a_value: float32 [8192, 16], replicated
- grad_b_value: float32 [16, 512], P(None, 'tensor')
All inputs are finite; a program needn't handle non-finite values.
Results may differ from a plain program's by a relative error of at most 0.015.
The roundings to bfloat16 on the way count: a program that leaves them out, or rounds other values in their place, can miss the bound.
Values may be sent and summed in bfloat16 or wider, within the bound.
A program may use at most 256 MiB of HBM per device.

v0:
```python
import math

import jax
import jax.numpy as jnp
from jax import lax
from jax.sharding import PartitionSpec as P

HD = 128
QUERY_PER_KV = 8


EPSILON = 1e-05
ADAPTER_SCALE = 2.0
ROPE_BASE = 500000.0


def normalize(own_rows, norm_gain):
    widened = own_rows.astype(jnp.float32)
    mean_square = jnp.mean(widened * widened, axis=-1, keepdims=True)
    return (widened * lax.rsqrt(mean_square + EPSILON) * norm_gain).astype(jnp.bfloat16)


def rotary(heads_block):
    sequence_length = heads_block.shape[0]
    half_dim = heads_block.shape[-1] // 2
    positions = jnp.arange(sequence_length, dtype=jnp.float32)[:, None]
    inv_freq = ROPE_BASE ** (-jnp.arange(half_dim, dtype=jnp.float32) / half_dim)
    angles = positions * inv_freq
    cosine = jnp.cos(angles)[:, None, :]
    sine_table = jnp.sin(angles)[:, None, :]
    front_half = heads_block[..., :half_dim].astype(jnp.float32)
    back_half = heads_block[..., half_dim:].astype(jnp.float32)
    turned = jnp.concatenate(
        [
            front_half * cosine - back_half * sine_table,
            back_half * cosine + front_half * sine_table,
        ],
        -1,
    )
    return turned.astype(jnp.bfloat16)


def attend(query_rows, key_heads, value_rows):
    sequence_length = query_rows.shape[0]
    kv_heads = key_heads.shape[1] // HD
    rot_queries = rotary(query_rows.reshape(sequence_length, kv_heads * QUERY_PER_KV, HD))
    rot_keys = rotary(key_heads.reshape(sequence_length, kv_heads, HD))
    split_values = value_rows.reshape(sequence_length, kv_heads, HD)
    causal = jnp.arange(sequence_length)[:, None] >= jnp.arange(sequence_length)[None, :]

    def one_head(head_index):
        q_head = lax.dynamic_index_in_dim(rot_queries, head_index, 1, keepdims=False)
        k_head = lax.dynamic_index_in_dim(rot_keys, head_index // QUERY_PER_KV, 1, keepdims=False)
        v_head = lax.dynamic_index_in_dim(
            split_values, head_index // QUERY_PER_KV, 1, keepdims=False
        )
        scores = jnp.dot(q_head, k_head.T, preferred_element_type=jnp.float32) * (
            1.0 / math.sqrt(HD)
        )
        scores = jnp.where(causal, scores, -1e30)
        row_max = jnp.max(scores, axis=-1, keepdims=True)
        weights = jnp.exp(scores - row_max)
        probabilities = (weights / jnp.sum(weights, axis=-1, keepdims=True)).astype(jnp.bfloat16)
        return jnp.dot(probabilities, v_head, preferred_element_type=jnp.float32).astype(
            jnp.bfloat16
        )

    per_head = lax.map(one_head, jnp.arange(kv_heads * QUERY_PER_KV, dtype=jnp.int32))
    return jnp.transpose(per_head, (1, 0, 2)).reshape(sequence_length, kv_heads * QUERY_PER_KV * HD)


def local(tokens, norm_gain, w_qkv, a_query, query_up_adapter, a_value, value_up_adapter, out_grad):
    normed_input = normalize(tokens[0], norm_gain)
    gathered = lax.all_gather(normed_input, "tensor", axis=0, tiled=True)
    sequence_length = gathered.shape[0]
    col_count = w_qkv.shape[1]
    projected = jnp.dot(
        gathered,
        lax.all_gather(w_qkv, ("dp", "fsdp"), axis=0, tiled=True),
        preferred_element_type=jnp.float32,
    )
    narrow_rank_rows = a_query.shape[1]
    down_projected = jnp.dot(
        gathered, jnp.concatenate([a_query, a_value], 1), preferred_element_type=jnp.float32
    ).astype(jnp.bfloat16)
    kv_local = col_count // ((QUERY_PER_KV + 2) * HD)
    grouped_queries = projected.reshape(sequence_length, kv_local, QUERY_PER_KV + 2, HD)
    query_rows = (
        grouped_queries[:, :, :QUERY_PER_KV].reshape(sequence_length, -1)
        + ADAPTER_SCALE
        * jnp.dot(
            down_projected[:, :narrow_rank_rows],
            query_up_adapter,
            preferred_element_type=jnp.float32,
        )
    ).astype(jnp.bfloat16)
    key_heads = (
        grouped_queries[:, :, QUERY_PER_KV].reshape(sequence_length, -1).astype(jnp.bfloat16)
    )
    value_rows = (
        grouped_queries[:, :, QUERY_PER_KV + 1].reshape(sequence_length, -1)
        + ADAPTER_SCALE
        * jnp.dot(
            down_projected[:, narrow_rank_rows:],
            value_up_adapter,
            preferred_element_type=jnp.float32,
        )
    ).astype(jnp.bfloat16)
    grad_rows = lax.all_to_all(out_grad[0], "tensor", split_axis=1, concat_axis=0, tiled=True)
    attended, pullback = jax.vjp(attend, query_rows, key_heads, value_rows)
    query_gradient, grad_keys, value_gradient = pullback(grad_rows)
    out_rows = lax.all_to_all(attended, "tensor", split_axis=0, concat_axis=1, tiled=True)
    query_up_gradient = ADAPTER_SCALE * jnp.einsum(
        "fb,fd->bd",
        down_projected[:, :narrow_rank_rows],
        query_gradient,
        preferred_element_type=jnp.float32,
    )
    value_up_gradient = ADAPTER_SCALE * jnp.einsum(
        "fb,fd->bd",
        down_projected[:, narrow_rank_rows:],
        value_gradient,
        preferred_element_type=jnp.float32,
    )
    middle_gradient = jnp.concatenate(
        [
            jnp.dot(query_gradient, query_up_adapter.T, preferred_element_type=jnp.float32),
            jnp.dot(value_gradient, value_up_adapter.T, preferred_element_type=jnp.float32),
        ],
        1,
    )
    mid_summed = lax.psum(middle_gradient, "tensor").astype(jnp.bfloat16)
    down_gradient = ADAPTER_SCALE * jnp.einsum(
        "uh,ux->hx", gathered, mid_summed, preferred_element_type=jnp.float32
    )
    down_gradient, query_up_gradient, value_up_gradient = lax.psum(
        (down_gradient, query_up_gradient, value_up_gradient), ("dp", "fsdp")
    )
    return (
        out_rows[None],
        down_gradient[:, :narrow_rank_rows],
        query_up_gradient,
        down_gradient[:, narrow_rank_rows:],
        value_up_gradient,
    )


def solution(mesh):
    return jax.shard_map(
        local,
        mesh=mesh,
        in_specs=(
            P(("dp", "fsdp"), "tensor", None),
            P(),
            P(("dp", "fsdp"), "tensor"),
            P(),
            P(None, "tensor"),
            P(),
            P(None, "tensor"),
            P(("dp", "fsdp"), "tensor", None),
        ),
        out_specs=(
            P(("dp", "fsdp"), "tensor", None),
            P(),
            P(None, "tensor"),
            P(),
            P(None, "tensor"),
        ),
        check_vma=False,
    )
```

profile of v0, /device:TPU:0, one launch (start us, length us, event | category | flops | bytes accessed | tf_op | source)
XLA Modules:
  0.0 691.3 jit_solution(7818503089707505698)
XLA Ops:
  7.2 2.8 fusion.62
  10.0 3.3 fusion.64
  17.5 6.3 all-to-all-start.1
  25.4 77.7 %all-to-all-done.1 = bf16[192,4,1024]{2,0,1:T(8,128)(2,1)S(1)} async-done(((bf16[192,4,1024]{2,0,1:T(8,128)(2,1)}), bf16[192,4,1024]{2,0,1:T(8,128)(2,1)S(1)}, u32[]{:S(2)}, u32[]{:S(2)}) %all-to-all-start.1) | async-done | bytes 1572896 | tf_op jit(solution)/shard_map/all_to_all | solution.py:109
  105.0 158.8 %all-gather.3.cloned.1.call-done = bf16[768,8192]{1,0:T(8,128)(2,1)} async-done(((bf16[192,8192]{1,0:T(8,128)(2,1)}), bf16[768,8192]{1,0:T(8,128)(2,1)}) %all-gather.3.cloned.1.call-update) | async-done | bytes 12582928 | tf_op jit(solution)/shard_map/all_gather | solution.py:74
  263.8 8.4 %convolution_convert_fusion.2 = bf16[768,32]{0,1:T(8,128)(2,1)S(1)} fusion(bf16[768,8192]{1,0:T(8,128)(2,1)} %all-gather.3.cloned.1.call-done, bf16[8192,16]{0,1:T(8,128)(2,1)S(1)} %copy-done.6, bf16[8192,16]{0,1:T(8,128)(2,1)S(1)} %copy-done.7), kind=kOutput, calls=%fused_computation.94 | convolution fusion | flops 403726336 | bytes 13156352 | tf_op jit(solution)/shard_map/dot_general | solution.py:83
  272.2 100.1 %all-gather.5.cloned.1.call-done = bf16[8192,1280]{1,0:T(8,128)(2,1)} async-done(((bf16[1024,1280]{1,0:T(8,128)(2,1)}), bf16[8192,1280]{1,0:T(8,128)(2,1)}) %all-gather.5.cloned.1.call-update) | async-done | bytes 20971536 | tf_op jit(solution)/shard_map/all_gather | solution.py:79
  372.3 22.9 %fusion.95 = f32[768,1280]{0,1:T(8,128)S(1)} fusion(bf16[768,8192]{1,0:T(8,128)(2,1)} %all-gather.3.cloned.1.call-done, bf16[8192,1280]{1,0:T(8,128)(2,1)} %all-gather.5.cloned.1.call-done), kind=kOutput, calls=%fused_computation.131 | convolution fusion | flops 16106127360 | bytes 37486592 | tf_op jit(solution)/shard_map/dot_general | solution.py:77
  407.8 85.5 %while.52 = (s32[]{:T(128)}, bf16[8,768,128]{2,1,0:T(8,128)(2,1)}, s32[8]{0:T(128)S(1)}, bf16[8,128,768]{2,1,0:T(8,128)(2,1)}, f32[8,768,768]{1,2,0:T(8,128)}, /...) while((s32[]{:T(128)}, bf16[8,768,128]{2,1,0:T(8,128)(2,1)}, ...), condition=%wide.region_5.6_spmd.clone, body=%wide.region_1.5_spmd.clone.sunk | while | flops 310344960 | bytes 20494060 | solution.py:68
  411.8 2.5 fusion.126
  422.4 2.5 fusion.126
  433.1 2.5 fusion.126
  443.7 2.6 fusion.126
  454.4 2.6 fusion.126
  465.1 2.6 fusion.126
  475.8 2.5 fusion.126
  486.5 2.5 fusion.126
  493.5 98.7 %while.53 = (s32[]{:T(128)}, bf16[768,8,128]{0,2,1:T(8,128)(2,1)S(1)}, bf16[768,1,128]{2,0,1:T(8,128)(2,1)}, s32[8]{0:T(128)S(1)}, bf16[8,768,128]{2,1,0:T(8,128...) while((s32[]{:T(128)}, ...), condition=%wide.region_9.10_spmd.clone, body=%wide.region_6.9_spmd.clone.sunk | while | flops 464683776 | bytes 17364168 | solution.py:68
  499.7 3.0 fusion.133
  511.9 3.0 fusion.133
  524.3 3.0 fusion.133
  528.1 2.5 fusion.134
  536.6 3.0 fusion.133
  548.9 3.0 fusion.133
  561.2 3.0 fusion.133
  573.5 3.0 fusion.133
  585.9 3.0 fusion.133
  595.4 20.2 %psum.28 = bf16[768,32]{0,1:T(8,128)(2,1)S(1)} all-reduce(f32[768,32]{0,1:T(8,128)S(1)} %pad_maximum_fusion.2), channel_id=1, replica_groups=mesh['dp'=4,'fsdp'=2,'tensor'=4] {'tensor'}, use_global_device_ids=true, to_apply=%region_10.11 | all-reduce | flops 24576 | bytes 147456 | tf_op jit(solution)/shard_map/psum | solution.py:132
  615.6 7.9 %convolution_multiply_fusion = f32[8192,32]{0,1:T(8,128)} fusion(bf16[768,8192]{1,0:T(8,128)(2,1)} %all-gather.3.cloned.1.call-done, bf16[768,32]{0,1:T(8,128)(2,1)S(1)} %psum.28), kind=kOutput, calls=%fused_computation.71 | convolution fusion | flops 402915328 | bytes 13680640 | tf_op jit(solution)/shard_map/uh,ux->hx/dot_general | solution.py:133
  626.7 3.6 all-to-all-start
  630.4 13.6 %psum.31 = f32[16,128]{1,0:T(8,128)} all-reduce(f32[16,128]{1,0:T(8,128)S(1)} %convolution_multiply_fusion.3), channel_id=1, replica_groups=mesh['dp'=4,'fsdp'=2,'tensor'=4] {'dp','fsdp'}, use_global_device_ids=true, to_apply=%region_13.14 | all-reduce | flops 2048 | bytes 16384 | tf_op jit(solution)/shard_map/psum | solution.py:136
  644.0 34.3 %all-reduce.5.cloned.1.call-done = (f32[8192,32]{0,1:T(8,128)}, f32[16,1024]{1,0:T(8,128)}) async-done(((f32[8192,32]{0,1:T(8,128)}, f32[16,1024]{1,0:T(8,128)}), (f32[8192,32]{0,1:T(8,128)}, f32[16,1024]{1,0:T(8,128)})) %all-reduce.5.cloned.1.call-update) | async-done | bytes 1114128 | tf_op jit(solution)/shard_map/psum | solution.py:136
  (256 shorter events, 154.0 us)
Async XLA Ops:
  7.2 392.2 %copy-start = (bf16[16,1024]{1,0:T(8,128)(2,1)S(1)}, bf16[16,1024]{1,0:T(8,128)(2,1)}, u32[]{:S(2)}) copy-start(bf16[16,1024]{1,0:T(8,128)(2,1)} %param.16) | copy-start | bytes 98308
  7.2 2.8 copy-start.1
  7.2 256.6 %all-gather.3.cloned.1.call-start = ((), (), s32[]{:S(2)}) async-start(), calls=%async_computation.2 | async-start | bytes 15728640 | tf_op jit(solution)/shard_map/all_gather | solution.py:74
  13.3 1.4 copy-start.3
  13.3 359.0 %all-gather.5.cloned.1.call-start = ((), (), s32[]{:S(2)}) async-start(), calls=%async_computation.3 | async-start | bytes 23592960 | tf_op jit(solution)/shard_map/all_gather | solution.py:79
  17.5 85.6 %all-to-all-start.1 = ((bf16[192,4,1024]{2,0,1:T(8,128)(2,1)}), bf16[192,4,1024]{2,0,1:T(8,128)(2,1)S(1)}, u32[]{:S(2)}, u32[]{:S(2)}) async-start(bf16[192,4,1024]{2,0,1:T(8,128)(2,1)} %copy.38), calls=%async_computation.1 | async-start | bytes 3145728 | tf_op jit(solution)/shard_map/all_to_all | solution.py:109
  23.9 654.4 %all-reduce.5.cloned.1.call-start = ((), (), s32[]{:S(2)}) async-start(), calls=%async_computation.4 | async-start | bytes 2228224 | tf_op jit(solution)/shard_map/psum | solution.py:136
  103.6 160.3 %copy-start.6 = (bf16[8192,16]{0,1:T(8,128)(2,1)S(1)}, bf16[8192,16]{0,1:T(8,128)(2,1)}, u32[]{:S(2)}) copy-start(bf16[8192,16]{0,1:T(8,128)(2,1)} %param.17) | copy-start | bytes 786436
  103.6 160.2 %copy-start.7 = (bf16[8192,16]{0,1:T(8,128)(2,1)S(1)}, bf16[8192,16]{0,1:T(8,128)(2,1)}, u32[]{:S(2)}) copy-start(bf16[8192,16]{0,1:T(8,128)(2,1)} %param.15) | copy-start | bytes 786436
  406.9 0.7 copy-start.9
  592.2 0.9 copy-start.2
  593.7 1.5 copy-start.5
  615.6 8.0 %copy-start.4 = (bf16[8,768,128]{2,1,0:T(8,128)(2,1)S(1)}, bf16[8,768,128]{2,1,0:T(8,128)(2,1)}, u32[]{:S(2)}) copy-start(bf16[8,768,128]{2,1,0:T(8,128)(2,1)} %get-tuple-element.648) | copy-start | bytes 4718596
  626.7 53.8 %all-to-all-start = ((bf16[4,192,1024]{2,1,0:T(8,128)(2,1)}), bf16[4,192,1024]{2,1,0:T(8,128)(2,1)S(1)}, u32[]{:S(2)}, u32[]{:S(2)}) async-start(bf16[4,192,1024]{2,1,0:T(8,128)(2,1)} %all_to_all.24), calls=%async_computation | async-start | bytes 3145728 | tf_op jit(solution)/shard_map/all_to_all | solution.py:112
  681.7 2.4 copy-start.8
Sparse Core Ops, SparseCore 0:
  13.4 250.3 all-gather.2
  265.7 106.5 all-gather.4
  623.7 54.5 all-reduce.4
where the time goes:
time: 693 us; the launch traced here: 691 us
  waiting for transfers between devices  372 us (54%)
  matrix products  121 us (17%)
  other arithmetic  66.7 us (10%)
  local copies, waits for them, and re-layouts  57.7 us (8%)
  blocking collectives  33.8 us (5%)
  loops' own time  16.5 us (2%)
  between operations  14.1 us (2%)
  starting transfers between devices  9.99 us (1%)
    all_gather x1, waiting for transfers between devices, local(): gathered = lax.all_gather(normed_input, 'tensor', axis=0, tiled=True)  159 us
    all_gather x1, waiting for transfers between devices, local(): lax.all_gather(w_qkv, ('dp', 'fsdp'), axis=0, tiled=True)  100 us
    all_to_all x1, waiting for transfers between devices, local(): lax.all_to_all(out_grad[0], 'tensor', split_axis=1, concat_axis=0, tiled=...  77.7 us
    dot_general x24, matrix products, one_head(): jnp.dot(probabilities, v_head, preferred_element_type=jnp.float32)  48.5 us
    psum x1, waiting for transfers between devices, local(): lax.psum((down_gradient, query_up_gradient, value_up_gradient), ('dp', 'f...  34.3 us
    dynamic_update_slice x24, other arithmetic, attend(): lax.map(one_head, jnp.arange(kv_heads * QUERY_PER_KV, dtype=jnp.int32))  31.9 us
    dot_general x16, matrix products, one_head(): jnp.dot(q_head, k_head.T, preferred_element_type=jnp.float32)  28.8 us
    dot_general x1, matrix products, local(): jnp.dot(gathered, lax.all_gather(w_qkv, ('dp', 'fsdp'), axis=0, tiled=Tru...  22.9 us
  transfers between devices with their start and end apart: 5, of which 4 were waited for; matrix products, arithmetic and copies ran while one was open for 2% of the time, Pallas kernels for 0%

commit v1 on v0

v1 whole, which is shorter than its diff:
```python
import functools
import math

import jax
import jax.numpy as jnp
from jax import lax
from jax.experimental import pallas as pl
from jax.experimental.pallas import tpu as pltpu
from jax.sharding import PartitionSpec as P

HD = 128
QUERY_PER_KV = 8


EPSILON = 1e-05
ADAPTER_SCALE = 2.0
ROPE_BASE = 500000.0


def normalize(own_rows, norm_gain):
    widened = own_rows.astype(jnp.float32)
    mean_square = jnp.mean(widened * widened, axis=-1, keepdims=True)
    return (widened * lax.rsqrt(mean_square + EPSILON) * norm_gain).astype(jnp.bfloat16)


def rotary_tables(sequence_length):
    half_dim = HD // 2
    positions = jnp.arange(sequence_length, dtype=jnp.float32)[:, None]
    inv_freq = ROPE_BASE ** (-jnp.arange(half_dim, dtype=jnp.float32) / half_dim)
    angles = positions * inv_freq
    cosine, sine = jnp.cos(angles), jnp.sin(angles)
    return jnp.concatenate([cosine, cosine], 1), jnp.concatenate([-sine, sine], 1)


def dot(a, b, dims):
    return lax.dot_general(a, b, (dims, ((), ())), preferred_element_type=jnp.float32)


def attention_kernel(
    block, q_ref, k_ref, v_ref, dq_ref, dv_ref, qup_ref, vup_ref, cos_ref, sin_ref, g_ref,
    out_ref, gbq_ref, gbv_ref, midq_ref, midv_ref,
    keys, values, value_grad, query_grad,
):
    group, head = pl.program_id(0), pl.program_id(1)
    heads = pl.num_programs(1)
    length = q_ref.shape[0]
    scale = 1.0 / math.sqrt(HD)

    @pl.when(head == 0)
    def _():
        k = k_ref[...].astype(jnp.bfloat16).astype(jnp.float32)
        keys[...] = (k * cos_ref[...] + pltpu.roll(k, HD // 2, 1) * sin_ref[...]).astype(jnp.bfloat16)
        values[...] = (
            v_ref[...] + ADAPTER_SCALE * dot(dv_ref[...], vup_ref[...], ((1,), (0,)))
        ).astype(jnp.bfloat16)
        value_grad[...] = jnp.zeros_like(value_grad)

    @pl.when((head == 0) & (group == 0))
    def _():
        midq_ref[...] = jnp.zeros_like(midq_ref)
        midv_ref[...] = jnp.zeros_like(midv_ref)

    for start in range(0, length, block):
        rows = pl.ds(start, block)
        reach = start + block
        q = (
            q_ref[rows, :] + ADAPTER_SCALE * dot(dq_ref[rows, :], qup_ref[...], ((1,), (0,)))
        ).astype(jnp.bfloat16).astype(jnp.float32)
        cosine, sine = cos_ref[rows, :], sin_ref[rows, :]
        turned = (q * cosine + pltpu.roll(q, HD // 2, 1) * sine).astype(jnp.bfloat16)
        k, v, g = keys[pl.ds(0, reach), :], values[pl.ds(0, reach), :], g_ref[rows, :]
        scores = dot(turned, k, ((1,), (1,))) * scale
        row = lax.broadcasted_iota(jnp.int32, scores.shape, 0) + start
        col = lax.broadcasted_iota(jnp.int32, scores.shape, 1)
        scores = jnp.where(row >= col, scores, -1e30)
        weights = jnp.exp(scores - jnp.max(scores, axis=-1, keepdims=True))
        wide = weights * (1.0 / jnp.sum(weights, axis=-1, keepdims=True))
        probabilities = wide.astype(jnp.bfloat16)
        out_ref[rows, :] = dot(probabilities, v, ((1,), (0,))).astype(jnp.bfloat16)
        value_grad[pl.ds(0, reach), :] += dot(probabilities, g, ((0,), (0,)))
        prob_grad = dot(g, v, ((1,), (1,)))
        inner = jnp.sum(prob_grad * wide, axis=-1, keepdims=True)
        score_grad = (wide * (prob_grad - inner) * scale).astype(jnp.bfloat16)
        turned_grad = dot(score_grad, k, ((1,), (0,))).astype(jnp.bfloat16).astype(jnp.float32)
        query_grad[rows, :] = (
            turned_grad * cosine - pltpu.roll(turned_grad, HD // 2, 1) * sine
        ).astype(jnp.bfloat16)

    gq = query_grad[...]
    gbq_ref[...] = ADAPTER_SCALE * dot(dq_ref[...], gq, ((0,), (0,)))
    midq_ref[...] += dot(gq, qup_ref[...], ((1,), (1,)))

    @pl.when(head == heads - 1)
    def _():
        gv = value_grad[...].astype(jnp.bfloat16)
        gbv_ref[...] = ADAPTER_SCALE * dot(dv_ref[...], gv, ((0,), (0,)))
        midv_ref[...] += dot(gv, vup_ref[...], ((1,), (1,)))


def attention(projected, down_q, down_v, query_up, value_up, grad_rows):
    length, cols = projected.shape
    rank = down_q.shape[1]
    per = QUERY_PER_KV + 2
    groups = cols // (per * HD)
    block = 256 if length % 256 == 0 else length
    cosine, sine = rotary_tables(length)
    heads = groups * QUERY_PER_KV
    whole = lambda shape: pl.BlockSpec(shape, lambda g, h: (0, 0))
    column = lambda n, index: pl.BlockSpec((n, HD), lambda g, h: (0, index(g, h)))
    by_head = lambda g, h: g * QUERY_PER_KV + h
    return pl.pallas_call(
        functools.partial(attention_kernel, block),
        grid=(groups, QUERY_PER_KV),
        in_specs=[
            column(length, lambda g, h: g * per + h),
            column(length, lambda g, h: g * per + QUERY_PER_KV),
            column(length, lambda g, h: g * per + QUERY_PER_KV + 1),
            whole((length, rank)),
            whole((length, rank)),
            column(rank, by_head),
            column(rank, lambda g, h: g),
            whole((length, HD)),
            whole((length, HD)),
            column(length, by_head),
        ],
        out_specs=[
            column(length, by_head),
            column(rank, by_head),
            column(rank, lambda g, h: g),
            whole((length, rank)),
            whole((length, rank)),
        ],
        out_shape=[
            jax.ShapeDtypeStruct((length, heads * HD), jnp.bfloat16),
            jax.ShapeDtypeStruct((rank, heads * HD), jnp.float32),
            jax.ShapeDtypeStruct((rank, groups * HD), jnp.float32),
            jax.ShapeDtypeStruct((length, rank), jnp.float32),
            jax.ShapeDtypeStruct((length, rank), jnp.float32),
        ],
        scratch_shapes=[
            pltpu.VMEM((length, HD), jnp.bfloat16),
            pltpu.VMEM((length, HD), jnp.bfloat16),
            pltpu.VMEM((length, HD), jnp.float32),
            pltpu.VMEM((length, HD), jnp.bfloat16),
        ],
        compiler_params=pltpu.CompilerParams(
            dimension_semantics=("arbitrary", "arbitrary"), vmem_limit_bytes=48 * 2**20
        ),
        cost_estimate=pl.CostEstimate(
            flops=10 * heads * length * length * HD,
            bytes_accessed=length * cols * 4 + 2 * length * heads * HD * 2,
            transcendentals=heads * length * length,
        ),
        name="attention",
    )(projected, projected, projected, down_q, down_v, query_up, value_up, cosine, sine, grad_rows)


def local(count, tokens, norm_gain, w_qkv, a_query, query_up_adapter, a_value, value_up_adapter, out_grad):
    own = normalize(tokens[0], norm_gain)
    own_rows = own.shape[0]
    rank = a_query.shape[1]
    place = lax.axis_index("tensor")
    weights = lax.all_gather(w_qkv, ("dp", "fsdp"), axis=0, tiled=True)
    adapters = jnp.concatenate([a_query, a_value], 1)
    grad_rows = lax.all_to_all(out_grad[0], "tensor", split_axis=1, concat_axis=0, tiled=True)

    down_own = jnp.dot(own, adapters, preferred_element_type=jnp.float32).astype(jnp.bfloat16)
    down_projected = lax.all_gather(down_own, "tensor", axis=0, tiled=True)

    upward, downward = [], []
    up_block = down_block = own
    for step in range(1, count):
        if step > 1 and step == count - 1:
            up_block, down_block, weights = lax.optimization_barrier((up_block, down_block, weights))
            upward[-1], downward[-1] = up_block, down_block
        up_block = lax.ppermute(up_block, "tensor", [(i, i + 1) for i in range(step - 1, count - 1)])
        down_block = lax.ppermute(down_block, "tensor", [(i, i - 1) for i in range(1, count - step + 1)])
        upward.append(up_block)
        downward.append(down_block)
    blocks = [
        jnp.dot(rows, weights, preferred_element_type=jnp.float32)
        for rows in upward[::-1] + [own] + downward
    ]
    window = (count - 1 - place) * own_rows
    projected = lax.dynamic_slice_in_dim(jnp.concatenate(blocks, 0), window, count * own_rows, 0)
    attended, query_up_gradient, value_up_gradient, mid_query, mid_value = attention(
        projected, down_projected[:, :rank], down_projected[:, rank:],
        query_up_adapter, value_up_adapter, grad_rows,
    )
    out_rows = lax.all_to_all(attended, "tensor", split_axis=0, concat_axis=1, tiled=True)
    mid_own = lax.psum_scatter(
        jnp.concatenate([mid_query, mid_value], 1), "tensor", scatter_dimension=0, tiled=True
    ).astype(jnp.bfloat16)
    down_gradient = ADAPTER_SCALE * jnp.einsum(
        "uh,ux->xh", own, mid_own, preferred_element_type=jnp.float32
    )
    down_gradient = lax.psum(down_gradient, ("dp", "fsdp", "tensor")).T
    query_up_gradient, value_up_gradient = lax.psum(
        (query_up_gradient, value_up_gradient), ("dp", "fsdp")
    )
    return (
        out_rows[None],
        down_gradient[:, :rank],
        query_up_gradient,
        down_gradient[:, rank:],
        value_up_gradient,
    )


def solution(mesh):
    return jax.shard_map(
        functools.partial(local, mesh.shape["tensor"]),
        mesh=mesh,
        in_specs=(
            P(("dp", "fsdp"), "tensor", None),
            P(),
            P(("dp", "fsdp"), "tensor"),
            P(),
            P(None, "tensor"),
            P(),
            P(None, "tensor"),
            P(("dp", "fsdp"), "tensor", None),
        ),
        out_specs=(
            P(("dp", "fsdp"), "tensor", None),
            P(),
            P(None, "tensor"),
            P(),
            P(None, "tensor"),
        ),
        check_vma=False,
    )
```

time: 693 us -> 611 us (0.88)
  blocking collectives: 33.8 us -> 101 us
  other arithmetic: 66.7 us -> 6.2 us
  matrix products: 121 us -> 74.4 us
  local copies, waits for them, and re-layouts: 57.7 us -> 20.6 us
  Pallas kernels: 0 us -> 31 us
  waiting for transfers between devices: 372 us -> 343 us
  loops' own time: 16.5 us -> 0 us
  starting transfers between devices: 9.99 us -> 20.1 us
    all_gather x2 -> x1, waiting for transfers between devices: 259 us -> 0.01 us  [local(): weights = lax.all_gather(w_qkv, ('dp', 'fsdp'), axis=0, tiled=True)]
    ppermute x0 -> x6, waiting for transfers between devices: none -> 145 us  [the longest x3 79.1 us: local(): lax.ppermute(down_block, 'tensor', [(i, i - 1) for i in range(1, count -...]
    psum x1 -> x2, waiting for transfers between devices: 34.3 us -> 178 us  [the longest x1 128 us: local(): down_gradient = lax.psum(down_gradient, ('dp', 'fsdp', 'tensor')).T]
    all_gather x0 -> x1, blocking collectives: none -> 85.9 us  [local(): down_projected = lax.all_gather(down_own, 'tensor', axis=0, tiled=True)]
    all_to_all x1, waiting for transfers between devices: 77.7 us -> 0.01 us  [local(): lax.all_to_all(out_grad[0], 'tensor', split_axis=1, concat_axis=0, tiled=...]
    dot_general x49 -> x9, matrix products: 121 us -> 74.4 us  [the longest x7 67.9 us: local(): jnp.dot(rows, weights, preferred_element_type=jnp.float32)]
    dynamic_update_slice x24 -> x0, other arithmetic: 31.9 us -> none  [attend(): lax.map(one_head, jnp.arange(kv_heads * QUERY_PER_KV, dtype=jnp.int32))]
    pallas_call x0 -> x1, Pallas kernels: none -> 31 us  [attention(): pl.pallas_call(functools.partial(attention_kernel, block), grid=(groups,...]
  transfers between devices with their start and end apart: 5 -> 12, of which waited for: 4 -> 7; matrix products, arithmetic and copies ran while one was open for 2% -> 14% of each run, Pallas kernels for 0% -> 0%
where the time goes in v1:
time: 611 us; the launch traced here: 610 us
  waiting for transfers between devices  343 us (56%)
  blocking collectives  101 us (17%)
  matrix products  74.4 us (12%)
  Pallas kernels  31 us (5%)
  local copies, waits for them, and re-layouts  20.6 us (3%)
  starting transfers between devices  20.1 us (3%)
  between operations  14.1 us (2%)
  other arithmetic  6.2 us (1%)
    psum x1, waiting for transfers between devices, local(): down_gradient = lax.psum(down_gradient, ('dp', 'fsdp', 'tensor')).T  128 us
    all_gather x1, blocking collectives, local(): down_projected = lax.all_gather(down_own, 'tensor', axis=0, tiled=True)  85.9 us
    ppermute x3, waiting for transfers between devices, local(): lax.ppermute(down_block, 'tensor', [(i, i - 1) for i in range(1, count -...  79.1 us
    dot_general x7, matrix products, local(): jnp.dot(rows, weights, preferred_element_type=jnp.float32)  67.9 us
    ppermute x3, waiting for transfers between devices, local(): lax.ppermute(up_block, 'tensor', [(i, i + 1) for i in range(step - 1, cou...  65.8 us
    psum x1, waiting for transfers between devices, local(): lax.psum((query_up_gradient, value_up_gradient), ('dp', 'fsdp'))  49.8 us
    pallas_call x1, Pallas kernels, attention(): pl.pallas_call(functools.partial(attention_kernel, block), grid=(groups,...  31 us
    unnamed x5, waiting for transfers between devices  20.3 us
  transfers between devices with their start and end apart: 12, of which 7 were waited for; matrix products, arithmetic and copies ran while one was open for 14% of the time, Pallas kernels for 0%

profile of v1, /device:TPU:0, one launch (start us, length us, event | category | flops | bytes accessed | tf_op | source)
XLA Modules:
  0.0 610.3 jit_solution(15705203789652585321)
XLA Ops:
  7.9 2.8 fusion.1
  10.7 1.6 fusion.3
  12.4 5.3 collective-permute-start
  19.0 65.8 %collective-permute-done = bf16[192,8192]{1,0:T(8,128)(2,1)S(1)} collective-permute-done((bf16[192,8192]{1,0:T(8,128)(2,1)S(1)}, bf16[192,8192]{1,0:T(8,128)(2,1)S(1)}, u32[]{:S(2)}, u32[]{:S(2)}) %collective-permute-start) | collective-permute-done | bytes 3145760 | tf_op jit(solution)/shard_map/ppermute | solution.py:176
  85.7 3.5 collective-permute-done.2
  89.1 1.8 copy-done.7
  92.2 1.6 copy-done.11
  93.9 68.0 %collective-permute-done.3 = bf16[192,8192]{1,0:T(8,128)(2,1)} collective-permute-done((bf16[192,8192]{1,0:T(8,128)(2,1)S(1)}, bf16[192,8192]{1,0:T(8,128)(2,1)}, u32[]{:S(2)}, u32[]{:S(2)}) %collective-permute-start.3) | collective-permute-done | bytes 3145760 | tf_op jit(solution)/shard_map/ppermute | solution.py:177
  161.8 2.3 collective-permute-start.4
  164.2 2.9 all_to_all.26
  168.7 3.6 all-to-all-start
  172.3 3.0 fusion.4
  175.3 85.9 %all-gather = bf16[4,192,32]{1,2,0:T(8,128)(2,1)S(1)} all-gather(bf16[1,192,32]{1,2,0:T(8,128)(2,1)S(1)} %fusion.4), channel_id=1, replica_groups=mesh['dp'=4,'fsdp'=2,'tensor'=4] {'tensor'}, dimensions={0}, use_global_device_ids=true | all-gather | bytes 61440 | tf_op jit(solution)/shard_map/all_gather | solution.py:168
  263.2 1.7 collective-permute-start.5
  265.0 10.5 %convolution_dynamic-update-slice_fusion.6 = f32[1344,1280]{1,0:T(8,128)S(1)} fusion(bf16[192,8192]{1,0:T(8,128)(2,1)} %collective-permute-done.4, bf16[8192,1280]{1,0:T(8,128)(2,1)} %all-gather.3.cloned.1.call-done), kind=kOutput, calls=%fused_computation.13 | convolution fusion | flops 4026531840 | bytes 25100288 | tf_op jit(solution)/shard_map/dot_general | solution.py:181
  275.5 9.4 %convolution_dynamic-update-slice_fusion.5 = f32[1344,1280]{1,0:T(8,128)S(1)} fusion(f32[1344,1280]{1,0:T(8,128)S(1)} %convolution_dynamic-update-slice_fusion.6, bf16[192,8192]{1,0:T(8,128)(2,1)S(1)} %copy-done.12, bf16[8192,1280]{1,0:T(8,128)(2,1)} %all-gather.3.cloned.1.call-done), kind=kOutput, calls=%fused_computation.12 | convolution fusion | flops 4026531840 | bytes 25100288 | tf_op jit(solution)/shard_map/dot_general | solution.py:181
  284.9 9.4 %convolution_dynamic-update-slice_fusion.4 = f32[1344,1280]{1,0:T(8,128)S(1)} fusion(f32[1344,1280]{1,0:T(8,128)S(1)} %convolution_dynamic-update-slice_fusion.5, bf16[192,8192]{1,0:T(8,128)(2,1)S(1)} %copy-done.10, bf16[8192,1280]{1,0:T(8,128)(2,1)} %all-gather.3.cloned.1.call-done), kind=kOutput, calls=%fused_computation.11 | convolution fusion | flops 4026531840 | bytes 25100288 | tf_op jit(solution)/shard_map/dot_general | solution.py:181
  294.3 9.4 %convolution_dynamic-update-slice_fusion.3 = f32[1344,1280]{1,0:T(8,128)S(1)} fusion(f32[1344,1280]{1,0:T(8,128)S(1)} %convolution_dynamic-update-slice_fusion.4, bf16[192,8192]{1,0:T(8,128)(2,1)S(1)} %copy-done.3, bf16[8192,1280]{1,0:T(8,128)(2,1)} %all-gather.3.cloned.1.call-done), kind=kOutput, calls=%fused_computation.10 | convolution fusion | flops 4026531840 | bytes 25100288 | tf_op jit(solution)/shard_map/dot_general | solution.py:181
  303.7 9.2 %convolution_dynamic-update-slice_fusion.2 = f32[1344,1280]{1,0:T(8,128)S(1)} fusion(f32[1344,1280]{1,0:T(8,128)S(1)} %convolution_dynamic-update-slice_fusion.3, bf16[192,8192]{1,0:T(8,128)(2,1)S(1)} %copy-done.8, bf16[8192,1280]{1,0:T(8,128)(2,1)} %all-gather.3.cloned.1.call-done), kind=kOutput, calls=%fused_computation.9 | convolution fusion | flops 4026531840 | bytes 25100288 | tf_op jit(solution)/shard_map/dot_general | solution.py:181
  313.0 10.7 %convolution_dynamic-update-slice_fusion.1 = f32[1344,1280]{1,0:T(8,128)S(1)} fusion(f32[1344,1280]{1,0:T(8,128)S(1)} %convolution_dynamic-update-slice_fusion.2, bf16[192,8192]{1,0:T(8,128)(2,1)} %collective-permute-done.3, bf16[8192,1280]{1,0:T(8,128)(2,1)} %all-gather.3.cloned.1.call-done), kind=kOutput, calls=%fused_computation.8 | convolution fusion | flops 4026531840 | bytes 25100288 | tf_op jit(solution)/shard_map/dot_general | solution.py:181
  323.7 7.6 %collective-permute-done.5 = bf16[192,8192]{1,0:T(8,128)(2,1)S(1)} collective-permute-done((bf16[192,8192]{1,0:T(8,128)(2,1)}, bf16[192,8192]{1,0:T(8,128)(2,1)S(1)}, u32[]{:S(2)}, u32[]{:S(2)}) %collective-permute-start.5) | collective-permute-done | bytes 3145760 | tf_op jit(solution)/shard_map/ppermute | solution.py:177
  331.4 9.2 %convolution_dynamic-update-slice_fusion = f32[1344,1280]{1,0:T(8,128)S(1)} fusion(f32[1344,1280]{1,0:T(8,128)S(1)} %convolution_dynamic-update-slice_fusion.1, bf16[192,8192]{1,0:T(8,128)(2,1)S(1)} %collective-permute-done.5, bf16[8192,1280]{1,0:T(8,128)(2,1)} %all-gather.3.cloned.1.call-done), kind=kOutput, calls=%fused_computation.7 | convolution fusion | flops 4026531840 | bytes 25100288 | tf_op jit(solution)/shard_map/dot_general | solution.py:181
  340.6 2.1 constant_dynamic-slice_fusion.q_ref.k_ref.v_ref
  343.5 31.0 %attention.1 = (bf16[768,1024]{1,0:T(8,128)(2,1)}, f32[16,1024]{1,0:T(8,128)}, f32[16,128]{1,0:T(8,128)S(1)}, f32[768,16]{1,0:T(8,128)S(1)}, f32[768,16]{1,0:T(8,128)S(1)}) custom-call(f32[768,1280]{1,0:T(8,128)} %constant_dynamic-slice_fusion.q_ref.k_ref.v_ref, f32[768,1280]{1,0:T(8,128)} %constant_dynamic-slice_fusion.q_ref.k_ref.v_ref, ...), custom_call_target="tpu_custom_call" | custom-call | flops 6039797760 | bytes 7077888 | tf_op jit(solution)/shard_map/attention/pallas_call | solution.py:111
  375.8 19.1 %reduce-scatter.4.cloned.1.call-done = f32[192,32]{1,0:T(8,128)} async-done(((f32[768,32]{1,0:T(8,128)}), f32[192,32]{1,0:T(8,128)}) %reduce-scatter.4.cloned.1.call-update) | async-done | bytes 24592
  395.8 3.6 fusion
  399.5 3.6 all-to-all-start.1
  403.6 14.8 %psum.23 = f32[16,128]{1,0:T(8,128)} all-reduce(f32[16,128]{1,0:T(8,128)S(1)} %get-tuple-element.20), channel_id=1, replica_groups=mesh['dp'=4,'fsdp'=2,'tensor'=4] {'dp','fsdp'}, use_global_device_ids=true, to_apply=%region_4.0 | all-reduce | flops 2048 | bytes 16384 | tf_op jit(solution)/shard_map/psum | solution.py:198
  418.4 128.2 %all-reduce.3.cloned.1.call-done = f32[8192,32]{0,1:T(8,128)} async-done(((f32[8192,32]{0,1:T(8,128)}), f32[8192,32]{0,1:T(8,128)}) %all-reduce.3.cloned.1.call-update) | async-done | bytes 1048592 | tf_op jit(solution)/shard_map/psum | solution.py:197
  546.6 2.2 fusion.13
  550.1 2.4 broadcast_in_dim.2
  552.5 49.8 %all-reduce.5.cloned.1.call-done = f32[16,1024]{1,0:T(8,128)} async-done(((f32[16,1024]{1,0:T(8,128)}), f32[16,1024]{1,0:T(8,128)}) %all-reduce.5.cloned.1.call-update) | async-done | bytes 65552 | tf_op jit(solution)/shard_map/psum | solution.py:198
  (54 shorter events, 14.1 us)
Async XLA Ops:
  7.2 3.6 copy-start.4
  7.2 154.7 %all-gather.3.cloned.1.call-start = ((), (), s32[]{:S(2)}) async-start(), calls=%async_computation.3 | async-start | bytes 23592960 | tf_op jit(solution)/shard_map/all_gather | solution.py:163
  12.4 5.3 copy-start.2
  12.4 159.9 %copy-start.5 = (bf16[8192,16]{0,1:T(8,128)(2,1)S(1)}, bf16[8192,16]{0,1:T(8,128)(2,1)}, u32[]{:S(2)}) copy-start(bf16[8192,16]{0,1:T(8,128)(2,1)} %param.13) | copy-start | bytes 786436
  12.4 159.9 %copy-start.6 = (bf16[8192,16]{0,1:T(8,128)(2,1)S(1)}, bf16[8192,16]{0,1:T(8,128)(2,1)}, u32[]{:S(2)}) copy-start(bf16[8192,16]{0,1:T(8,128)(2,1)} %param.11) | copy-start | bytes 786436
  12.4 72.4 %collective-permute-start = (bf16[192,8192]{1,0:T(8,128)(2,1)S(1)}, bf16[192,8192]{1,0:T(8,128)(2,1)S(1)}, u32[]{:S(2)}, u32[]{:S(2)}) collective-permute-start(bf16[192,8192]{1,0:T(8,128)(2,1)S(1)} %fusion.3), channel_id=1, source_target_pairs={{0,1},{1,2},{2,3},{4,5},{5,6},{6,7},{8,9},{9,10},{10,11},{12,13},{... | collective-permute-start | bytes 9437192 | tf_op jit(solution)/shard_map/ppermute | solution.py:176
  17.7 71.5 %collective-permute-start.2 = (bf16[192,8192]{1,0:T(8,128)(2,1)S(1)}, bf16[192,8192]{1,0:T(8,128)(2,1)S(1)}, u32[]{:S(2)}, u32[]{:S(2)}) collective-permute-start(bf16[192,8192]{1,0:T(8,128)(2,1)S(1)} %fusion.3), channel_id=1, source_target_pairs={{1,0},{2,1},{3,2},{5,4},{6,5},{7,6},{9,8},{10,9},{11,10},{13,12},{... | collective-permute-start | bytes 9437192 | tf_op jit(solution)/shard_map/ppermute | solution.py:177
  84.8 7.4 %copy-start.9 = (bf16[192,8192]{1,0:T(8,128)(2,1)}, bf16[192,8192]{1,0:T(8,128)(2,1)S(1)}, u32[]{:S(2)}) copy-start(bf16[192,8192]{1,0:T(8,128)(2,1)S(1)} %collective-permute-done) | copy-start | bytes 9437188
  84.8 7.4 %collective-permute-start.1 = (bf16[192,8192]{1,0:T(8,128)(2,1)S(1)}, bf16[192,8192]{1,0:T(8,128)(2,1)S(1)}, u32[]{:S(2)}, u32[]{:S(2)}) collective-permute-start(bf16[192,8192]{1,0:T(8,128)(2,1)S(1)} %collective-permute-done), channel_id=1, source_target_pairs={{1,2},{2,3},{5,6},{6,7},{9,10},{10,11},{13,14},{14,15},{17,18},{18... | collective-permute-start | bytes 9437192 | tf_op jit(solution)/shard_map/ppermute | solution.py:176
  89.1 1.8 copy-start.7
  90.9 70.9 %collective-permute-start.3 = (bf16[192,8192]{1,0:T(8,128)(2,1)S(1)}, bf16[192,8192]{1,0:T(8,128)(2,1)}, u32[]{:S(2)}, u32[]{:S(2)}) collective-permute-start(bf16[192,8192]{1,0:T(8,128)(2,1)S(1)} %collective-permute-done.2), channel_id=1, source_target_pairs={{1,0},{2,1},{5,4},{6,5},{9,8},{10,9},{13,12},{14,13},{17,16},{18,1... | collective-permute-start | bytes 9437192 | tf_op jit(solution)/shard_map/ppermute | solution.py:177
  92.2 1.6 copy-start.11
  161.8 103.1 %collective-permute-start.4 = (bf16[192,8192]{1,0:T(8,128)(2,1)}, bf16[192,8192]{1,0:T(8,128)(2,1)}, u32[]{:S(2)}, u32[]{:S(2)}) collective-permute-start(bf16[192,8192]{1,0:T(8,128)(2,1)} %copy-done.11), channel_id=1, source_target_pairs={{2,3},{6,7},{10,11},{14,15},{18,19},{22,23},{26,27},{30,31}} | collective-permute-start | bytes 9437192 | tf_op jit(solution)/shard_map/ppermute | solution.py:176
  168.7 174.1 %all-to-all-start = ((bf16[192,4,1024]{2,0,1:T(8,128)(2,1)}), bf16[192,4,1024]{2,0,1:T(8,128)(2,1)S(1)}, u32[]{:S(2)}, u32[]{:S(2)}) async-start(bf16[192,4,1024]{2,0,1:T(8,128)(2,1)} %copy.22), calls=%async_computation | async-start | bytes 3145728 | tf_op jit(solution)/shard_map/all_to_all | solution.py:165
  172.2 222.6 %reduce-scatter.4.cloned.1.call-start = ((), (), s32[]{:S(2)}) async-start(), calls=%async_computation.6 | async-start | bytes 491520
  263.2 12.3 %copy-start.12 = (bf16[192,8192]{1,0:T(8,128)(2,1)S(1)}, bf16[192,8192]{1,0:T(8,128)(2,1)}, u32[]{:S(2)}) copy-start(bf16[192,8192]{1,0:T(8,128)(2,1)} %copy-done.11) | copy-start | bytes 9437188
  263.2 68.1 %collective-permute-start.5 = (bf16[192,8192]{1,0:T(8,128)(2,1)}, bf16[192,8192]{1,0:T(8,128)(2,1)S(1)}, u32[]{:S(2)}, u32[]{:S(2)}) collective-permute-start(bf16[192,8192]{1,0:T(8,128)(2,1)} %collective-permute-done.3), channel_id=1, source_target_pairs={{1,0},{5,4},{9,8},{13,12},{17,16},{21,20},{25,24},{29,28}} | collective-permute-start | bytes 9437192 | tf_op jit(solution)/shard_map/ppermute | solution.py:177
  275.5 9.4 %copy-start.10 = (bf16[192,8192]{1,0:T(8,128)(2,1)S(1)}, bf16[192,8192]{1,0:T(8,128)(2,1)}, u32[]{:S(2)}) copy-start(bf16[192,8192]{1,0:T(8,128)(2,1)} %copy-done.9) | copy-start | bytes 9437188
  284.9 9.4 %copy-start.3 = (bf16[192,8192]{1,0:T(8,128)(2,1)S(1)}, bf16[192,8192]{1,0:T(8,128)(2,1)}, u32[]{:S(2)}) copy-start(bf16[192,8192]{1,0:T(8,128)(2,1)} %copy-done.2) | copy-start | bytes 9437188
  294.3 9.4 %copy-start.8 = (bf16[192,8192]{1,0:T(8,128)(2,1)S(1)}, bf16[192,8192]{1,0:T(8,128)(2,1)}, u32[]{:S(2)}) copy-start(bf16[192,8192]{1,0:T(8,128)(2,1)} %copy-done.7) | copy-start | bytes 9437188
  340.6 2.1 copy-start.1
  342.7 0.8 copy-start
  375.7 170.9 %all-reduce.3.cloned.1.call-start = ((), (), s32[]{:S(2)}) async-start(), calls=%async_computation.4 | async-start | bytes 2097152 | tf_op jit(solution)/shard_map/psum | solution.py:197
  399.5 149.4 %all-to-all-start.1 = ((bf16[4,192,1024]{2,1,0:T(8,128)(2,1)}), bf16[4,192,1024]{2,1,0:T(8,128)(2,1)S(1)}, u32[]{:S(2)}, u32[]{:S(2)}) async-start(bf16[4,192,1024]{2,1,0:T(8,128)(2,1)} %bitcast.6), calls=%async_computation.1 | async-start | bytes 3145728 | tf_op jit(solution)/shard_map/all_to_all | solution.py:190
  403.0 199.2 %all-reduce.5.cloned.1.call-start = ((), (), s32[]{:S(2)}) async-start(), calls=%async_computation.5 | async-start | bytes 131072 | tf_op jit(solution)/shard_map/psum | solution.py:198
Sparse Core Ops, SparseCore 0:
  9.9 110.1 all-gather.2
  375.8 18.9 reduce-scatter.3
  400.1 146.5 all-reduce.2
  550.1 52.1 all-reduce.4
